TPU v7x, 32 devices: a whole 2x2x4 slice. The times are simulated.
32 devices in a mesh: ens: 2 (over y), gx: 16 (over z, x, core).
Axes of the slice: x: 2, y: 2, z: 4, core: 2. Of those that a mesh axis runs over, the one named last changes fastest.
Arguments:
- model_state: float32 [8, 4, 320, 2560], P('ens', None, 'gx'), parts along dimension 0, may hold values from -6 to 6
- driving: float32 [8, 4, 320, 2560], P('ens', None, 'gx'), parts along dimension 0, may hold values from -12 to 12
- mode_east: int32 [30], replicated, may hold values from 1 to 60, as said below
- mode_north: int32 [30], replicated, may hold values from 1 to 60, as said below
- level_class: int32 [4], replicated, may hold values from 0 to 7
- nudge_table: float32 [8, 4], replicated, may hold values from 0.05 to 0.5
Outputs:
- nudged: float32 [8, 4, 320, 2560], P('ens', None, 'gx'), parts along dimension 0
- residual_log: float32 [8, 4], P('ens'), parts along dimension 0
There are 2 independent parts, one for each index of `ens`. A program takes and returns all parts, laid end to end along the dimension named above; an argument that names none is the same for every part. Nothing has to cross between parts.
Inputs may be any that keep to these rules, and one draw needn't show every extreme that they name: `mode_east`: 30 distinct wavenumbers in increasing order, the first 1 and the last 60. `mode_north`: 30 distinct wavenumbers in increasing order, the first 1 and the last 60.
All inputs are finite; a program needn't handle non-finite values.
Results may differ from a plain program's by a relative error of at most 0.0001.
Values sent between devices are 32-bit elements; how exact they have to be, the bound alone decides.
A program may use at most 128 MiB of HBM per device.

v0:
```python
import jax
import jax.numpy as jnp
from jax import lax
from jax.sharding import PartitionSpec as P

ITERS = 4
DIFFUSION = 0.24


def extended_2(cells, sides, width):
    for axis, dim in sides:
        count = lax.axis_size(axis)
        ends = count - 1
        head = lax.slice_in_dim(cells, 0, width, axis=dim)
        tail = lax.slice_in_dim(cells, cells.shape[dim] - width, cells.shape[dim], axis=dim)
        cells = jnp.concatenate(
            [
                lax.ppermute(tail, axis, [(i, (i + 1) % count) for i in range(ends)]),
                cells,
                lax.ppermute(head, axis, [((i + 1) % count, i) for i in range(ends)]),
            ],
            axis=dim,
        )
    return cells


def sine_table(wavenums, first_cell, span_cols, grid_cells):
    places = first_cell + lax.iota(jnp.int32, span_cols) + 1
    phases = wavenums[:, None] * places[None, :] % (2 * (grid_cells + 1))
    return jnp.sin(phases.astype(jnp.float32) * (jnp.pi / (grid_cells + 1)))


def laplace(extended):
    centre = extended[:, :, 1:-1]
    padded = jnp.pad(centre, ((0, 0), (0, 0), (0, 0), (1, 1)))
    return (
        extended[:, :, 2:]
        + extended[:, :, :-2]
        + padded[:, :, :, 2:]
        + padded[:, :, :, :-2]
        - 4.0 * centre
    )


def local(model_state, driving, mode_east, mode_north, level_class, nudge_table):
    fields, levels, columns, north_cells = model_state.shape
    tiles = lax.axis_size("gx")
    first_col = lax.axis_index("gx") * columns
    total_east = columns * tiles
    scale_norm = 4.0 / ((total_east + 1) * (north_cells + 1))
    cell_count = float(levels * total_east * north_cells)
    table_north = sine_table(mode_north, 0, north_cells, north_cells)
    table_own = sine_table(mode_east, first_col, columns, total_east)
    one_hot = (level_class[:, None] == lax.iota(jnp.int32, nudge_table.shape[0])[None, :]).astype(
        jnp.float32
    )
    weights = jnp.dot(one_hot, nudge_table, precision=lax.Precision.HIGHEST).T[:, :, None, None]
    records = []
    extended = extended_2(model_state, (("gx", 2),), ITERS)
    for substep in range(ITERS):
        reach_now = ITERS - substep
        current = extended[:, :, reach_now : reach_now + columns]
        along_north = jnp.dot(
            (driving - current).reshape(-1, north_cells),
            table_north.T,
            precision=lax.Precision.HIGHEST,
        )
        along_north = along_north.reshape(fields, levels, columns, -1)
        mode_partial_value = (
            jnp.einsum("flxb,ax->flab", along_north, table_own, precision=lax.Precision.HIGHEST)
            * scale_norm
        )
        coeffs = lax.psum(mode_partial_value, "gx")
        lead_col = first_col - (reach_now - 1)
        span_cols = columns + 2 * (reach_now - 1)
        table_wide = sine_table(mode_east, lead_col, span_cols, total_east)
        global_col = lead_col + lax.iota(jnp.int32, span_cols)
        inside = ((global_col >= 0) & (global_col < total_east))[None, None, :, None]
        partial_value = jnp.einsum(
            "flab,ax->flxb", coeffs, table_wide, precision=lax.Precision.HIGHEST
        )
        rebuild_span_cols = table_wide.shape[1]
        flat = jnp.dot(
            partial_value.reshape(-1, partial_value.shape[-1]),
            table_north,
            precision=lax.Precision.HIGHEST,
        )
        updated = (
            extended[:, :, 1:-1]
            + flat.reshape(fields, levels, rebuild_span_cols, north_cells) * weights
            + DIFFUSION * laplace(extended)
        )
        extended = jnp.where(inside, updated, 0.0)
        current = extended[:, :, reach_now - 1 : reach_now - 1 + columns]
        remain = driving - current
        squares = jnp.sum(remain * remain, axis=(1, 2, 3))
        records.append(lax.psum(squares, "gx"))
    stacked = jnp.stack(records)
    return (current, jnp.sqrt(stacked / cell_count))


def solution(mesh):
    return jax.shard_map(
        local,
        mesh=mesh,
        in_specs=(P("ens", None, "gx", None), P("ens", None, "gx", None), P(), P(), P(), P()),
        out_specs=(P("ens", None, "gx", None), P("ens", None)),
        check_vma=False,
    )
```

profile of v0, /device:TPU:0, one launch (start us, length us, event | category | flops | bytes accessed | tf_op | source)
XLA Modules:
  0.0 384.4 jit_solution(12978652984436395358)
XLA Ops:
  0.7 3.1 copy.8
  3.8 1.9 copy-done.2
  5.7 1.2 fusion.219
  6.9 3.3 collective-permute-start
  10.2 1.3 collective-permute-start.1
  13.4 3.6 sub.42
  17.0 4.7 %fusion.29 = f32[4,4,20,30]{3,2,1,0:T(8,128)S(1)} fusion(f32[4,4,20,2560]{3,1,2,0:T(4,128)S(1)} %sub.42, s32[2560]{0:T(1024)S(1)} %iota_add_fusion, s32[30]{0:T(128)S(1)} %copy-done.7), kind=kOutput, calls=%fused_computation.49 | convolution fusion | flops 295603200 | bytes 3325560 | tf_op jit(solution)/shard_map/dot_general | solution.py:63
  23.1 66.8 %psum.56 = f32[4,4,30,30]{3,1,0,2:T(4,128)S(1)} all-reduce(f32[4,4,30,30]{3,1,0,2:T(4,128)} %bitcast.73), channel_id=1, replica_groups=mesh['ens'=2,'gx'=16] {'gx'}, use_global_device_ids=true, to_apply=%region_0.1 | all-reduce | flops 14400 | bytes 115200 | tf_op jit(solution)/shard_map/psum | solution.py:73
  91.6 3.2 pad_maximum_fusion
  95.7 6.8 %fusion.5 = f32[4,4,26,2560]{3,2,1,0:T(8,128)S(1)} fusion(f32[4,4,26,2560]{3,2,1,0:T(8,128)S(1)} %slice.106, f32[4,4,28,2560]{3,2,1,0:T(8,128)S(1)} %pad_maximum_fusion, f32[4,4,26,30]{3,2,1,0:T(8,128)S(1)} %convolution_bitcast_fusion, f32[4,4]{1,0:T(4,128)S(1)} %copy.11, pred[26]{0:T(512)(128)(4,1)S(1)} %compare_and_fusion, s32[2560]{0:T(1024)S(1)} %iota_add_fusion, ...), kind=kOutput, calls=%fused_computation.7 | convolution fusion | flops 394726400 | bytes 17099730 | tf_op jit(solution)/shard_map/dot_general | solution.py:83
  102.6 5.5 %fusion.32 = f32[4,4,20,30]{3,2,1,0:T(8,128)S(1)} fusion(f32[4,4,20,2560]{3,1,2,0:T(4,128)S(1)} %copy-done.1, f32[4,4,26,2560]{3,2,1,0:T(8,128)S(1)} %fusion.5, s32[2560]{0:T(1024)S(1)} %iota_add_fusion, s32[30]{0:T(128)S(1)} %copy-done.7), kind=kOutput, calls=%fused_computation.55 | convolution fusion | flops 296422400 | bytes 7260160 | tf_op jit(solution)/shard_map/dot_general | solution.py:63
  108.1 2.5 slice.109
  111.9 60.4 %psum.57 = f32[4,4,30,30]{3,1,0,2:T(4,128)S(1)} all-reduce(f32[4,4,30,30]{3,1,0,2:T(4,128)} %bitcast.74), channel_id=1, replica_groups=mesh['ens'=2,'gx'=16] {'gx'}, use_global_device_ids=true, to_apply=%region_1.2 | all-reduce | flops 14400 | bytes 115200 | tf_op jit(solution)/shard_map/psum | solution.py:73
  173.5 10.2 %fusion.12 = f32[4,4,24,2560]{3,2,1,0:T(8,128)S(1)} fusion(f32[4,4,24,2560]{3,2,1,0:T(8,128)} %slice.109, f32[4,4,24,30]{3,2,1,0:T(8,128)S(1)} %convolution_bitcast_fusion.3, f32[4,4,26,2560]{3,2,1,0:T(8,128)} %copy-done.5, f32[4,4]{1,0:T(4,128)S(1)} %copy.11, pred[24]{0:T(512)(128)(4,1)} %compare_and_fusion.1, s32[2560]{0:T(1024)S(1)} %iota_add_fusion, ...), kind=kOutput, calls=%fused_computation.19 | convolution fusion | flops 364416000 | bytes 15785168 | tf_op jit(solution)/shard_map/dot_general | solution.py:83
  183.7 5.2 %fusion.33 = f32[4,4,20,30]{3,2,1,0:T(8,128)S(1)} fusion(f32[4,4,20,2560]{3,1,2,0:T(4,128)S(1)} %copy-done.1, f32[4,4,24,2560]{3,2,1,0:T(8,128)S(1)} %fusion.12, s32[2560]{0:T(1024)S(1)} %iota_add_fusion, s32[30]{0:T(128)S(1)} %copy-done.7), kind=kOutput, calls=%fused_computation.56 | convolution fusion | flops 296422400 | bytes 7257720 | tf_op jit(solution)/shard_map/dot_general | solution.py:63
  189.0 2.5 slice.113
  192.8 60.8 %psum.58 = f32[4,4,30,30]{3,1,0,2:T(4,128)S(1)} all-reduce(f32[4,4,30,30]{3,1,0,2:T(4,128)} %bitcast.75), channel_id=1, replica_groups=mesh['ens'=2,'gx'=16] {'gx'}, use_global_device_ids=true, to_apply=%region_2.3 | all-reduce | flops 14400 | bytes 115200 | tf_op jit(solution)/shard_map/psum | solution.py:73
  254.7 9.9 %fusion.13 = f32[4,4,22,2560]{3,2,1,0:T(8,128)S(1)} fusion(f32[4,4,22,2560]{3,2,1,0:T(8,128)} %slice.113, f32[4,4,22,30]{3,2,1,0:T(8,128)S(1)} %convolution_bitcast_fusion.2, f32[4,4,24,2560]{3,2,1,0:T(8,128)} %copy-done.3, f32[4,4]{1,0:T(4,128)S(1)} %copy.11, pred[22]{0:T(512)(128)(4,1)} %compare_and_fusion.2, s32[2560]{0:T(1024)S(1)} %iota_add_fusion, ...), kind=kOutput, calls=%fused_computation.20 | convolution fusion | flops 334105600 | bytes 14470606 | tf_op jit(solution)/shard_map/dot_general | solution.py:83
  264.6 5.2 %fusion.31 = f32[4,4,20,30]{3,2,1,0:T(8,128)S(1)} fusion(f32[4,4,20,2560]{3,1,2,0:T(4,128)S(1)} %copy-done.1, s32[2560]{0:T(1024)S(1)} %iota_add_fusion, s32[30]{0:T(128)S(1)} %copy-done.7, f32[4,4,22,2560]{3,2,1,0:T(8,128)S(1)} %fusion.13), kind=kOutput, calls=%fused_computation.54 | convolution fusion | flops 296422400 | bytes 6930040 | tf_op jit(solution)/shard_map/dot_general | solution.py:63
  269.9 2.4 slice.117
  273.6 60.6 %psum.59 = f32[4,4,30,30]{3,1,0,2:T(4,128)S(1)} all-reduce(f32[4,4,30,30]{3,1,0,2:T(4,128)} %bitcast.76), channel_id=1, replica_groups=mesh['ens'=2,'gx'=16] {'gx'}, use_global_device_ids=true, to_apply=%region_3.4 | all-reduce | flops 14400 | bytes 115200 | tf_op jit(solution)/shard_map/psum | solution.py:73
  334.7 15.7 %multiply_reduce_fusion.2 = (f32[4]{0:T(128)S(1)}, f32[4]{0:T(128)S(1)}, f32[4]{0:T(128)S(1)}, f32[4]{0:T(128)S(1)}, f32[4,4,20,2560]{3,2,1,0:T(8,128)S(1)}) fusion(f32[4,4,26,2560]{3,2,1,0:T(8,128)} %copy-done.5, f32[4,4,20,2560]{3,1,2,0:T(4,128)S(1)} %copy-done.1, f32[4,4,24,2560]{3,2,1,0:T(8,128)} %copy-done.3, f32[4,4,22,2560]{3,2,1,0:T(8,128)} %copy-done.4, ...), kind=kOutput, calls=%fused_computation.53 | convolution fusion | flops 313625600 | bytes 26263308 | tf_op jit(solution)/shard_map/dot_general | solution.py:83
  350.4 3.8 copy.19
  354.2 29.5 %all-reduce.4 = (f32[1,4]{1,0:T(1,128)S(1)}, f32[1,4]{1,0:T(1,128)S(1)}, f32[1,4]{1,0:T(1,128)S(1)}, f32[1,4]{1,0:T(1,128)S(1)}) all-reduce(f32[1,4]{1,0:T(1,128)S(1)} %bitcast.80, f32[1,4]{1,0:T(1,128)S(1)} %bitcast.79, f32[1,4]{1,0:T(1,128)S(1)} %bitcast.78, f32[1,4]{1,0:T(1,128)S(1)} %bitcast.77), channel_id=1, replica_groups=mesh['ens'=2,'gx'=16] {'gx'}, use_global_device_ids=true, to_apply=%region_11.12 | all-reduce | flops 16 | bytes 128 | tf_op jit(solution)/shard_map/psum | solution.py:97
  (44 shorter events, 13.3 us)
Async XLA Ops:
  0.6 12.5 %copy-start = (f32[8,4]{0,1:T(4,128)S(1)}, f32[8,4]{0,1:T(4,128)}, u32[]{:S(2)}) copy-start(f32[8,4]{0,1:T(4,128)} %param.11) | copy-start | bytes 388
  0.6 12.4 %copy-start.8 = (s32[4]{0:T(128)S(1)}, s32[4]{0:T(128)}, u32[]{:S(2)}) copy-start(s32[4]{0:T(128)} %param.10) | copy-start | bytes 52
  0.7 12.7 %copy-start.1 = (f32[4,4,20,2560]{3,1,2,0:T(4,128)S(1)}, f32[4,4,20,2560]{3,1,2,0:T(4,128)}, u32[]{:S(2)}) copy-start(f32[4,4,20,2560]{3,1,2,0:T(4,128)} %param.7) | copy-start | bytes 9830404
  3.8 1.9 copy-start.2
  6.9 84.6 %collective-permute-start = (f32[4,4,4,2560]{3,2,1,0:T(4,128)}, f32[4,4,4,2560]{3,2,1,0:T(4,128)}, u32[]{:S(2)}, u32[]{:S(2)}) collective-permute-start(f32[4,4,4,2560]{3,2,1,0:T(4,128)} %get-tuple-element.12), channel_id=1, source_target_pairs={{0,1},{1,2},{2,3},{3,4},{4,5},{5,6},{6,7},{7,8},{8,9},{9,10},{10,1... | collective-permute-start | bytes 1966088 | tf_op jit(solution)/shard_map/ppermute | solution.py:18
  10.2 81.4 %collective-permute-start.1 = (f32[4,4,4,2560]{3,2,1,0:T(4,128)}, f32[4,4,4,2560]{3,2,1,0:T(4,128)}, u32[]{:S(2)}, u32[]{:S(2)}) collective-permute-start(f32[4,4,4,2560]{3,2,1,0:T(4,128)} %get-tuple-element.13), channel_id=1, source_target_pairs={{1,0},{2,1},{3,2},{4,3},{5,4},{6,5},{7,6},{8,7},{9,8},{10,9},{11,1... | collective-permute-start | bytes 1966088 | tf_op jit(solution)/shard_map/ppermute | solution.py:20
  13.4 3.6 copy-start.7
  17.0 4.8 %copy-start.6 = (s32[30]{0:T(128)S(1)}, s32[30]{0:T(128)}, u32[]{:S(2)}) copy-start(s32[30]{0:T(128)} %param.8) | copy-start | bytes 364
  102.6 5.5 %copy-start.5 = (f32[4,4,26,2560]{3,2,1,0:T(8,128)}, f32[4,4,26,2560]{3,2,1,0:T(8,128)S(1)}, u32[]{:S(2)}) copy-start(f32[4,4,26,2560]{3,2,1,0:T(8,128)S(1)} %fusion.5) | copy-start | bytes 12779524
  183.7 5.2 %copy-start.3 = (f32[4,4,24,2560]{3,2,1,0:T(8,128)}, f32[4,4,24,2560]{3,2,1,0:T(8,128)S(1)}, u32[]{:S(2)}) copy-start(f32[4,4,24,2560]{3,2,1,0:T(8,128)S(1)} %fusion.12) | copy-start | bytes 11796484
  264.6 5.3 %copy-start.4 = (f32[4,4,22,2560]{3,2,1,0:T(8,128)}, f32[4,4,22,2560]{3,2,1,0:T(8,128)S(1)}, u32[]{:S(2)}) copy-start(f32[4,4,22,2560]{3,2,1,0:T(8,128)S(1)} %fusion.13) | copy-start | bytes 10813444
where the time goes:
time: 392 us; the launch traced here: 384 us
  blocking collectives  278 us (71%)
  matrix products  68.8 us (18%)
  local copies, waits for them, and re-layouts  21.9 us (6%)
  other arithmetic  10.1 us (3%)
  starting transfers between devices  4.53 us (1%)
    psum x4, blocking collectives, local(): coeffs = lax.psum(mode_partial_value, 'gx')  248 us
    dot_general x4, matrix products, local(): jnp.dot(partial_value.reshape(-1, partial_value.shape[-1]), table_north,...  42.6 us
    psum x1, blocking collectives, local(): records.append(lax.psum(squares, 'gx'))  29.5 us
    dot_general x4, matrix products, local(): jnp.dot((driving - current).reshape(-1, north_cells), table_north.T, prec...  20.7 us
    unnamed x24, local copies, waits for them, and re-layouts  12.3 us
    slice x4, local copies, waits for them, and re-layouts, local(): extended[:, :, 1:-1]  8.25 us
  transfers between devices with their start and end apart: 2, of which 0 were waited for; matrix products, arithmetic and copies ran while one was open for 3% of the time, Pallas kernels for 0%

commit v1 on v0

--- a/solution.py
+++ b/solution.py
@@ -70,7 +70,12 @@
             jnp.einsum("flxb,ax->flab", along_north, table_own, precision=lax.Precision.HIGHEST)
             * scale_norm
         )
-        coeffs = lax.psum(mode_partial_value, "gx")
+
+        def define_state(sheet):
+            moved = lax.all_gather(sheet, axis_name="gx").sum(axis=0)
+            return moved
+
+        coeffs = define_state(mode_partial_value)
         lead_col = first_col - (reach_now - 1)
         span_cols = columns + 2 * (reach_now - 1)
         table_wide = sine_table(mode_east, lead_col, span_cols, total_east)

time: 392 us -> 358 us (0.913)
  blocking collectives: 278 us -> 237 us
  other arithmetic: 10.1 us -> 21.6 us
    psum x4 -> x0, blocking collectives: 248 us -> none  [local(): coeffs = lax.psum(mode_partial_value, 'gx')]
    all_gather x0 -> x4, blocking collectives: none -> 207 us  [define_state(): moved = lax.all_gather(sheet, axis_name='gx').sum(axis=0)]
    reduce_sum x0 -> x4, other arithmetic: none -> 11.9 us  [define_state(): moved = lax.all_gather(sheet, axis_name='gx').sum(axis=0)]
  transfers between devices with their start and end apart: 2 -> 2, of which waited for: 0 -> 0; matrix products, arithmetic and copies ran while one was open for 3% -> 4% of each run, Pallas kernels for 0% -> 0%
where the time goes in v1:
time: 358 us; the launch traced here: 352 us
  blocking collectives  237 us (66%)
  matrix products  68.3 us (19%)
  other arithmetic  21.6 us (6%)
  local copies, waits for them, and re-layouts  19.1 us (5%)
  starting transfers between devices  4.55 us (1%)
    all_gather x4, blocking collectives, define_state(): moved = lax.all_gather(sheet, axis_name='gx').sum(axis=0)  207 us
    dot_general x4, matrix products, local(): jnp.dot(partial_value.reshape(-1, partial_value.shape[-1]), table_north,...  42.6 us
    psum x1, blocking collectives, local(): records.append(lax.psum(squares, 'gx'))  30.6 us
    dot_general x4, matrix products, local(): jnp.dot((driving - current).reshape(-1, north_cells), table_north.T, prec...  20.8 us
    reduce_sum x4, other arithmetic, define_state(): moved = lax.all_gather(sheet, axis_name='gx').sum(axis=0)  11.9 us
    unnamed x24, local copies, waits for them, and re-layouts  8.86 us
    slice x4, local copies, waits for them, and re-layouts, local(): extended[:, :, 1:-1]  8.25 us
  transfers between devices with their start and end apart: 2, of which 0 were waited for; matrix products, arithmetic and copies ran while one was open for 4% of the time, Pallas kernels for 0%

profile of v1, /device:TPU:0, one launch (start us, length us, event | category | flops | bytes accessed | tf_op | source)
XLA Modules:
  0.0 352.2 jit_solution(11070941493842399604)
XLA Ops:
  0.7 3.1 copy.36
  6.9 3.3 collective-permute-start
  12.9 3.6 %sub.42 = f32[4,4,20,2560]{3,1,2,0:T(4,128)S(1)} subtract(f32[4,4,20,2560]{3,1,2,0:T(4,128)S(1)} %copy-done.2, f32[4,4,20,2560]{3,1,2,0:T(4,128)} %param.6) | non-fusion elementwise | flops 819200 | bytes 9830400 | tf_op jit(solution)/shard_map/sub | solution.py:64
  16.5 4.7 %fusion.29 = f32[4,4,20,30]{3,2,1,0:T(8,128)S(1)} fusion(f32[4,4,20,2560]{3,1,2,0:T(4,128)S(1)} %sub.42, s32[2560]{0:T(1024)S(1)} %iota_add_fusion, s32[30]{0:T(128)S(1)} %copy-done.8), kind=kOutput, calls=%fused_computation.49 | convolution fusion | flops 295603200 | bytes 3325560 | tf_op jit(solution)/shard_map/dot_general | solution.py:63
  22.0 53.3 %all-gather = f32[64,4,30,30]{3,1,2,0:T(4,128)} all-gather(f32[4,4,30,30]{3,1,2,0:T(4,128)S(1)} %copy.40), channel_id=2, replica_groups=mesh['ens'=2,'gx'=16] {'gx'}, dimensions={0}, use_global_device_ids=true | all-gather | bytes 979200 | tf_op jit(solution)/shard_map/all_gather | solution.py:75
  75.3 3.0 reduce_sum.72
  80.0 3.2 pad_maximum_fusion
  84.1 6.8 %fusion.5 = f32[4,4,26,2560]{3,2,1,0:T(8,128)S(1)} fusion(f32[4,4,26,2560]{3,2,1,0:T(8,128)S(1)} %slice.106, f32[4,4,28,2560]{3,2,1,0:T(8,128)S(1)} %pad_maximum_fusion, f32[4,4,26,30]{3,2,1,0:T(8,128)S(1)} %convolution_bitcast_fusion, f32[4,4]{1,0:T(4,128)S(1)} %copy.42, pred[26]{0:T(512)(128)(4,1)S(1)} %compare_and_fusion, s32[2560]{0:T(1024)S(1)} %iota_add_fusion, ...), kind=kOutput, calls=%fused_computation.7 | convolution fusion | flops 394726400 | bytes 17099730 | tf_op jit(solution)/shard_map/dot_general | solution.py:88
  91.0 5.6 %fusion.32 = f32[4,4,20,30]{3,2,1,0:T(8,128)S(1)} fusion(f32[4,4,20,2560]{3,1,2,0:T(4,128)S(1)} %copy-done.2, f32[4,4,26,2560]{3,2,1,0:T(8,128)S(1)} %fusion.5, s32[2560]{0:T(1024)S(1)} %iota_add_fusion, s32[30]{0:T(128)S(1)} %copy-done.8), kind=kOutput, calls=%fused_computation.55 | convolution fusion | flops 296422400 | bytes 7260160 | tf_op jit(solution)/shard_map/dot_general | solution.py:63
  96.6 2.5 slice.109
  99.8 48.5 %all-gather.1 = f32[64,4,30,30]{3,1,2,0:T(4,128)} all-gather(f32[4,4,30,30]{3,1,2,0:T(4,128)S(1)} %copy.44), channel_id=3, replica_groups=mesh['ens'=2,'gx'=16] {'gx'}, dimensions={0}, use_global_device_ids=true | all-gather | bytes 979200 | tf_op jit(solution)/shard_map/all_gather | solution.py:75
  148.3 3.0 reduce_sum.73
  152.4 10.2 %fusion.12 = f32[4,4,24,2560]{3,2,1,0:T(8,128)S(1)} fusion(f32[4,4,24,2560]{3,2,1,0:T(8,128)} %slice.109, f32[4,4,24,30]{3,2,1,0:T(8,128)S(1)} %convolution_bitcast_fusion.3, f32[4,4,26,2560]{3,2,1,0:T(8,128)} %copy-done.6, f32[4,4]{1,0:T(4,128)S(1)} %copy.42, pred[24]{0:T(512)(128)(4,1)} %compare_and_fusion.1, s32[2560]{0:T(1024)S(1)} %iota_add_fusion, ...), kind=kOutput, calls=%fused_computation.19 | convolution fusion | flops 364416000 | bytes 15785168 | tf_op jit(solution)/shard_map/dot_general | solution.py:88
  162.6 5.2 %fusion.33 = f32[4,4,20,30]{3,2,1,0:T(8,128)S(1)} fusion(f32[4,4,20,2560]{3,1,2,0:T(4,128)S(1)} %copy-done.2, f32[4,4,24,2560]{3,2,1,0:T(8,128)S(1)} %fusion.12, s32[2560]{0:T(1024)S(1)} %iota_add_fusion, s32[30]{0:T(128)S(1)} %copy-done.8), kind=kOutput, calls=%fused_computation.56 | convolution fusion | flops 296422400 | bytes 7257720 | tf_op jit(solution)/shard_map/dot_general | solution.py:63
  167.9 2.5 slice.113
  171.0 54.7 %all-gather.2 = f32[64,4,30,30]{3,1,2,0:T(4,128)} all-gather(f32[4,4,30,30]{3,1,2,0:T(4,128)S(1)} %copy.48), channel_id=4, replica_groups=mesh['ens'=2,'gx'=16] {'gx'}, dimensions={0}, use_global_device_ids=true | all-gather | bytes 979200 | tf_op jit(solution)/shard_map/all_gather | solution.py:75
  225.8 3.0 reduce_sum.74
  229.2 9.9 %fusion.13 = f32[4,4,22,2560]{3,2,1,0:T(8,128)S(1)} fusion(f32[4,4,22,2560]{3,2,1,0:T(8,128)} %slice.113, f32[4,4,22,30]{3,2,1,0:T(8,128)S(1)} %convolution_bitcast_fusion.2, f32[4,4,24,2560]{3,2,1,0:T(8,128)} %copy-done.4, f32[4,4]{1,0:T(4,128)S(1)} %copy.42, pred[22]{0:T(512)(128)(4,1)} %compare_and_fusion.2, s32[2560]{0:T(1024)S(1)} %iota_add_fusion, ...), kind=kOutput, calls=%fused_computation.20 | convolution fusion | flops 334105600 | bytes 14470606 | tf_op jit(solution)/shard_map/dot_general | solution.py:88
  239.1 5.2 %fusion.31 = f32[4,4,20,30]{3,2,1,0:T(8,128)S(1)} fusion(f32[4,4,20,2560]{3,1,2,0:T(4,128)S(1)} %copy-done.2, s32[2560]{0:T(1024)S(1)} %iota_add_fusion, s32[30]{0:T(128)S(1)} %copy-done.8, f32[4,4,22,2560]{3,2,1,0:T(8,128)S(1)} %fusion.13), kind=kOutput, calls=%fused_computation.54 | convolution fusion | flops 296422400 | bytes 6930040 | tf_op jit(solution)/shard_map/dot_general | solution.py:63
  247.5 50.4 %all-gather.3 = f32[64,4,30,30]{3,1,2,0:T(4,128)} all-gather(f32[4,4,30,30]{3,1,2,0:T(4,128)S(1)} %copy.52), channel_id=5, replica_groups=mesh['ens'=2,'gx'=16] {'gx'}, dimensions={0}, use_global_device_ids=true | all-gather | bytes 979200 | tf_op jit(solution)/shard_map/all_gather | solution.py:75
  297.9 3.0 reduce_sum.75
  301.3 15.6 %multiply_reduce_fusion.2 = (f32[4]{0:T(128)S(1)}, f32[4]{0:T(128)S(1)}, f32[4]{0:T(128)S(1)}, f32[4]{0:T(128)S(1)}, f32[4,4,20,2560]{3,2,1,0:T(8,128)S(1)}) fusion(f32[4,4,26,2560]{3,2,1,0:T(8,128)} %copy-done.6, f32[4,4,20,2560]{3,1,2,0:T(4,128)S(1)} %copy-done.2, f32[4,4,24,2560]{3,2,1,0:T(8,128)} %copy-done.4, f32[4,4,22,2560]{3,2,1,0:T(8,128)} %copy-done.5, ...), kind=kOutput, calls=%fused_computation.53 | convolution fusion | flops 313625600 | bytes 26263308 | tf_op jit(solution)/shard_map/dot_general | solution.py:88
  317.0 3.8 %copy.56 = f32[4,4,20,2560]{3,1,2,0:T(4,128)} copy(f32[4,4,20,2560]{3,2,1,0:T(8,128)S(1)} %get-tuple-element.18) | data formatting | bytes 6553600
  320.8 30.6 %all-reduce.4 = (f32[1,4]{1,0:T(1,128)S(1)}, f32[1,4]{1,0:T(1,128)S(1)}, f32[1,4]{1,0:T(1,128)S(1)}, f32[1,4]{1,0:T(1,128)S(1)}) all-reduce(f32[1,4]{1,0:T(1,128)S(1)} %bitcast.80, f32[1,4]{1,0:T(1,128)S(1)} %bitcast.79, f32[1,4]{1,0:T(1,128)S(1)} %bitcast.78, f32[1,4]{1,0:T(1,128)S(1)} %bitcast.77), channel_id=1, replica_groups=mesh['ens'=2,'gx'=16] {'gx'}, use_global_device_ids=true, to_apply=%region_11.12 | all-reduce | flops 16 | bytes 128 | tf_op jit(solution)/shard_map/psum | solution.py:102
  (52 shorter events, 16.2 us)
Async XLA Ops:
  0.6 12.0 %copy-start = (f32[8,4]{0,1:T(4,128)S(1)}, f32[8,4]{0,1:T(4,128)}, u32[]{:S(2)}) copy-start(f32[8,4]{0,1:T(4,128)} %param.11) | copy-start | bytes 388
  0.6 12.0 %copy-start.9 = (s32[4]{0:T(128)S(1)}, s32[4]{0:T(128)}, u32[]{:S(2)}) copy-start(s32[4]{0:T(128)} %param.10) | copy-start | bytes 52
  0.7 12.2 %copy-start.2 = (f32[4,4,20,2560]{3,1,2,0:T(4,128)S(1)}, f32[4,4,20,2560]{3,1,2,0:T(4,128)}, u32[]{:S(2)}) copy-start(f32[4,4,20,2560]{3,1,2,0:T(4,128)} %param.7) | copy-start | bytes 9830404
  3.8 1.9 copy-start.3
  6.9 73.0 %collective-permute-start = (f32[4,4,4,2560]{3,2,1,0:T(4,128)}, f32[4,4,4,2560]{3,2,1,0:T(4,128)}, u32[]{:S(2)}, u32[]{:S(2)}) collective-permute-start(f32[4,4,4,2560]{3,2,1,0:T(4,128)} %get-tuple-element.16), channel_id=1, source_target_pairs={{0,1},{1,2},{2,3},{3,4},{4,5},{5,6},{6,7},{7,8},{8,9},{9,10},{10,1... | collective-permute-start | bytes 1966088 | tf_op jit(solution)/shard_map/ppermute | solution.py:18
  10.2 69.8 %collective-permute-start.1 = (f32[4,4,4,2560]{3,2,1,0:T(4,128)}, f32[4,4,4,2560]{3,2,1,0:T(4,128)}, u32[]{:S(2)}, u32[]{:S(2)}) collective-permute-start(f32[4,4,4,2560]{3,2,1,0:T(4,128)} %get-tuple-element.17), channel_id=1, source_target_pairs={{1,0},{2,1},{3,2},{4,3},{5,4},{6,5},{7,6},{8,7},{9,8},{10,9},{11,1... | collective-permute-start | bytes 1966088 | tf_op jit(solution)/shard_map/ppermute | solution.py:20
  12.9 3.6 %copy-start.8 = (s32[30]{0:T(128)S(1)}, s32[30]{0:T(128)}, u32[]{:S(2)}) copy-start(s32[30]{0:T(128)} %param.9) | copy-start | bytes 364
  16.5 4.8 %copy-start.7 = (s32[30]{0:T(128)S(1)}, s32[30]{0:T(128)}, u32[]{:S(2)}) copy-start(s32[30]{0:T(128)} %param.8) | copy-start | bytes 364
  91.0 5.7 %copy-start.6 = (f32[4,4,26,2560]{3,2,1,0:T(8,128)}, f32[4,4,26,2560]{3,2,1,0:T(8,128)S(1)}, u32[]{:S(2)}) copy-start(f32[4,4,26,2560]{3,2,1,0:T(8,128)S(1)} %fusion.5) | copy-start | bytes 12779524
  162.6 5.2 %copy-start.4 = (f32[4,4,24,2560]{3,2,1,0:T(8,128)}, f32[4,4,24,2560]{3,2,1,0:T(8,128)S(1)}, u32[]{:S(2)}) copy-start(f32[4,4,24,2560]{3,2,1,0:T(8,128)S(1)} %fusion.12) | copy-start | bytes 11796484
  239.1 5.3 %copy-start.5 = (f32[4,4,22,2560]{3,2,1,0:T(8,128)}, f32[4,4,22,2560]{3,2,1,0:T(8,128)S(1)}, u32[]{:S(2)}) copy-start(f32[4,4,22,2560]{3,2,1,0:T(8,128)S(1)} %fusion.13) | copy-start | bytes 10813444
  247.5 53.8 %copy-start.10 = (pred[20]{0:T(512)(128)(4,1)S(1)}, pred[20]{0:T(512)(128)(4,1)}, u32[]{:S(2)}) copy-start(pred[20]{0:T(512)(128)(4,1)} %compare_and_fusion.3) | copy-start | bytes 64
  301.3 50.6 %copy-start.1 = (f32[8,4]{0,1:T(4,128)S(1)}, f32[8,4]{0,1:T(4,128)}, u32[]{:S(2)}) copy-start(f32[8,4]{0,1:T(4,128)} %param.11) | copy-start | bytes 388
